TPU v7x, 32 devices: a whole 2x2x4 slice. The times are simulated.
32 devices in a mesh: tp: 4 (over z), dp: 8 (over y, x, core).
Axes of the slice: x: 2, y: 2, z: 4, core: 2. Of those that a mesh axis runs over, the one named last changes fastest.
Arguments:
- design: float32 [65536, 1536], P('dp', 'tp')
- target: float32 [65536], P('dp')
- ridge: float32 [], replicated
Outputs:
- output 1: float32 [1536], replicated
- output 2: float32 [65536], P('dp')
All inputs are finite; a program needn't handle non-finite values.
Results may differ from a plain program's by a relative error of at most 0.001.
Values sent between devices are 32-bit elements.
A program may use at most 1 GiB of HBM per device.

v0:
```python
import functools
import jax
import jax.numpy as jnp
from jax import lax
from jax.experimental import pallas as pl
from jax.experimental.pallas import tpu as pltpu
from jax.sharding import PartitionSpec as P

HIGHEST = lax.Precision.HIGHEST
F32 = jnp.float32
SUB, HALF, PANEL, BLOCK, EXTRA = 16, 128, 256, 384, 128
PAIR = 2 * BLOCK
MESH = pl.DeviceIdType.MESH
MIB = 1024 * 1024


def dot(a, b, dims=((1,), (0,))):
    return lax.dot_general(a, b, (dims, ((), ())), precision=HIGHEST, preferred_element_type=F32)


def row_blocks(work, r):
    return work[r:r + SUB, :HALF], work[r:r + SUB, HALF:]


def lanes(block, col0):
    return [jnp.broadcast_to(block[:, col0 + c:col0 + c + 1], (SUB, HALF)) for c in range(SUB)]


def invert_factor(work, inv_ref):
    rows = lax.broadcasted_iota(jnp.int32, (SUB, HALF), 0)
    left, right = row_blocks(work, 0)
    for r in range(0, HALF, SUB):
        more = r + SUB < HALF
        cols = lanes(left, r)
        if more:
            next_left, next_right = row_blocks(work, r + SUB)
            below = lanes(next_left, r)
        pivots = cols[0]
        for p in range(SUB):
            inv = 1.0 / cols[p][p:p + 1, :]
            fac = jnp.where(rows > p, cols[p] * inv, 0.0)
            left_row, right_row = left[p:p + 1, :], right[p:p + 1, :]
            left, right = left - fac * left_row, right - fac * right_row
            if more:
                low = below[p] * inv
                next_left, next_right = next_left - low * left_row, next_right - low * right_row
            for c in range(p + 1, SUB):
                entry = cols[c][p:p + 1, :]
                cols[c] = cols[c] - fac * entry
                if more:
                    below[c] = below[c] - low * entry
            pivots = jnp.where(rows == p, cols[p], pivots)
        scale = lax.rsqrt(pivots)
        left, right = left * scale, right * scale
        inv_ref[r:r + SUB, :] = right
        if r + 2 * SUB < HALF:
            upd = dot(left, jnp.concatenate([left, right], axis=1), ((0,), (0,)))
            work[r + 2 * SUB:, :] = work[r + 2 * SUB:, :] - upd[r + 2 * SUB:, :]
        if more:
            left, right = next_left, next_right


def eye(n):
    rows = lax.broadcasted_iota(jnp.int32, (n, n), 0)
    return jnp.where(rows == lax.broadcasted_iota(jnp.int32, (n, n), 1), 1.0, 0.0).astype(F32)


def factor(up, inv, work, small, n):
    panels = n // PANEL
    first, carry = small.at[0], small.at[1]

    def step(t, _):
        k, odd = t // 2, lax.rem(t, 2)
        r0 = pl.multiple_of(t * HALF, HALF)
        r1 = pl.multiple_of(t * HALF + HALF * (1 - odd), HALF)
        work[:, :HALF] = up[pl.ds(r0, HALF), pl.ds(r0, HALF)]
        work[:, HALF:] = eye(HALF)
        invert_factor(work, first)

        @pl.when(odd == 0)
        def _():
            w1 = first[...]
            inv[k] = jnp.zeros((PANEL, PANEL), F32)
            inv[k, :HALF, :HALF] = w1
            u12 = dot(w1, up[pl.ds(r0, HALF), pl.ds(r1, HALF)])
            both = dot(u12, jnp.concatenate([u12, w1], axis=1), ((0,), (0,)))
            up[pl.ds(r1, HALF), pl.ds(r1, HALF)] = up[pl.ds(r1, HALF), pl.ds(r1, HALF)] - both[:, :HALF]
            carry[...] = both[:, HALF:]

        @pl.when(odd == 1)
        def _():
            w2 = first[...]
            inv[k, HALF:, HALF:] = w2
            inv[k, HALF:, :HALF] = -dot(w2, carry[...])

        for kk in range(panels):
            @pl.when(t == 2 * kk + 1)
            def _():
                a, b = kk * PANEL, (kk + 1) * PANEL
                up[a:b, b:] = dot(inv[kk], up[a:b, b:])
                for i in range(kk + 1, panels):
                    c = i * PANEL
                    up[c:c + PANEL, c:] = up[c:c + PANEL, c:] - dot(up[a:b, c:c + PANEL], up[a:b, c:], ((0,), (0,)))
        return 0

    lax.fori_loop(0, 2 * panels, step, 0)


def places():
    z, dp = lax.axis_index('tp'), lax.axis_index('dp')
    core, x, y = lax.rem(dp, 2), lax.rem(dp // 2, 2), dp // 4
    return z, dp, core, x, y


def z_peers(z):
    return (z + 1 - 2 * lax.rem(z, 2), z + 2 - 4 * (z // 2), 3 - z)


def plane_peers(z, dp, core, x, y):
    return ({'tp': z, 'dp': dp + 1 - 2 * core}, {'tp': z, 'dp': dp + 2 - 4 * x}, {'tp': z, 'dp': dp + 4 - 8 * y})


def meet(peers):
    barrier = pltpu.get_barrier_semaphore()
    for peer in peers:
        pl.semaphore_signal(barrier, inc=1, device_id=peer, device_id_type=MESH)
    pl.semaphore_wait(barrier, len(peers))


def starter(send_sem, recv_sem):
    count = [0]

    def start(src, dst, peer):
        i = count[0]
        count[0] += 1
        copy = pltpu.make_async_remote_copy(src_ref=src, dst_ref=dst, send_sem=send_sem.at[i], recv_sem=recv_sem.at[i], device_id=peer, device_id_type=MESH)
        copy.start()
        return copy

    return start


def at(base, size):
    return pl.ds(pl.multiple_of(base, 8), size)


def spans(rows, core, x, y):
    half, quart, eighth, sixt = rows // 2, rows // 4, rows // 8, rows // 16
    a1, b1 = x * eighth, quart + y * eighth
    return core * half, a1, b1, a1 + y * sixt, b1 + x * sixt


def plane_scatter(rows, part, acc, got, start, peers, where):
    _, _, core, x, y = where
    core_peer, x_peer, y_peer = peers
    half, quart, eighth, sixt = rows // 2, rows // 4, rows // 8, rows // 16
    own, a1, b1, a2, b2 = spans(rows, core, x, y)
    got_core, got_a, got_b, got_a2, got_b2 = got
    copy = start(part.at[at((1 - core) * half, half)], got_core, core_peer)
    yield
    copy.wait()
    acc[...] = part[at(own, half)] + got_core[...]
    copies = [start(acc.at[at((1 - x) * eighth, eighth)], got_a, x_peer), start(acc.at[at(quart + (1 - y) * eighth, eighth)], got_b, y_peer)]
    yield
    copies[0].wait()
    acc[at(a1, eighth)] = acc[at(a1, eighth)] + got_a[...]
    copies[1].wait()
    acc[at(b1, eighth)] = acc[at(b1, eighth)] + got_b[...]
    copies = [start(acc.at[at(a1 + (1 - y) * sixt, sixt)], got_a2, y_peer), start(acc.at[at(b1 + (1 - x) * sixt, sixt)], got_b2, x_peer)]
    yield
    copies[0].wait()
    acc[at(a2, sixt)] = acc[at(a2, sixt)] + got_a2[...]
    copies[1].wait()
    acc[at(b2, sixt)] = acc[at(b2, sixt)] + got_b2[...]


def plane_gather(rows, full, start, peers, where):
    _, _, core, x, y = where
    core_peer, x_peer, y_peer = peers
    half, eighth, sixt = rows // 2, rows // 8, rows // 16
    own, a1, b1, a2, b2 = spans(rows, core, x, y)
    for sizes in (((a2, sixt, y_peer), (b2, sixt, x_peer)), ((a1, eighth, x_peer), (b1, eighth, y_peer)), ((0, half, core_peer),)):
        copies = []
        for base, size, peer in sizes:
            ref = full.at[:, at(own + base, size)]
            copies.append(start(ref, ref, peer))
        yield
        for copy in copies:
            copy.wait()


def in_turn(chunks):
    chunks = list(chunks)
    while chunks:
        chunks = [chunk for chunk in chunks if next(chunk, chunks) is not chunks]


def wait_all(copies):
    for copy in copies:
        copy.wait()


def sum_chunk(rows, part, acc, full, got, got_z, start, peers, z_peer, where):
    z, _, core, x, y = where
    yield from plane_scatter(rows, part, acc, got, start, peers, where)
    own, _, _, a2, b2 = spans(rows, core, x, y)
    share = rows // 64
    copies = []
    for k, piece in enumerate((a2, b2)):
        for j, peer in enumerate(z_peer):
            copies.append(start(acc.at[at(piece + peer['tp'] * share, share)], got_z.at[2 * j + k], peer))
    yield
    wait_all(copies)
    copies = []
    for k, piece in enumerate((a2, b2)):
        mine = piece + z * share
        full[0, at(own + mine, share)] = (acc[at(mine, share)] + got_z[k]) + (got_z[2 + k] + got_z[4 + k])
        ref = full.at[0, at(own + mine, share)]
        copies += [start(ref, ref, peer) for peer in z_peer]
    yield
    wait_all(copies)
    yield from plane_gather(rows, full, start, peers, where)


CHUNKS = 4


def sum_kernel(rows, part, out, acc, full, g0, g1, g2, g3, g4, got_z, send_sem, recv_sem, out_sem):
    where = places()
    z, dp = where[:2]
    peers = plane_peers(*where)
    z_peer = [{'tp': p, 'dp': dp} for p in z_peers(z)]
    meet(list(peers) + z_peer)
    start = starter(send_sem, recv_sem)
    size = rows // CHUNKS
    in_turn(sum_chunk(size, part.at[c * size:(c + 1) * size], acc.at[c], full.at[:, c * size:(c + 1) * size],
                      [g.at[c] for g in (g0, g1, g2, g3, g4)], got_z.at[c], start, peers, z_peer, where) for c in range(CHUNKS))
    copy = pltpu.make_async_copy(full, out, out_sem)
    copy.start()
    copy.wait()


def stack_kernel(rows, part, out, acc, mine, g0, g1, g2, g3, g4, send_sem, recv_sem, out_sem):
    where = places()
    z, dp, core, x, y = where
    peers = plane_peers(*where)
    z_peer = [{'tp': p, 'dp': dp} for p in z_peers(z)]
    meet(list(peers) + z_peer)
    start = starter(send_sem, recv_sem)
    in_turn([plane_scatter(rows, part, acc.at[0], [g.at[0] for g in (g0, g1, g2, g3, g4)], start, peers, where)])
    _, _, _, a2, b2 = spans(rows, core, x, y)
    sixt = rows // 16
    mine[z, :sixt] = acc[0, at(a2, sixt)]
    mine[z, sixt:] = acc[0, at(b2, sixt)]
    wait_all([start(mine.at[z], mine.at[z], peer) for peer in z_peer])
    copy = pltpu.make_async_copy(mine, out, out_sem)
    copy.start()
    copy.wait()


def spread_kernel(rows, mine, out, full, send_sem, recv_sem, out_sem):
    where = places()
    _, _, core, x, y = where
    peers = plane_peers(*where)
    meet(peers)
    own, _, _, a2, b2 = spans(rows, core, x, y)
    sixt = rows // 16
    full[:, at(own + a2, sixt)] = mine[:, :sixt]
    full[:, at(own + b2, sixt)] = mine[:, sixt:]
    start = starter(send_sem, recv_sem)
    in_turn(plane_gather(rows, full.at[2 * c:2 * c + 2], start, peers, where) for c in range(2))
    copy = pltpu.make_async_copy(full, out, out_sem)
    copy.start()
    copy.wait()


def scatter_scratch(chunks, rows):
    return [pltpu.VMEM((chunks, rows // d, BLOCK), F32) for d in (2, 8, 8, 16, 16)]


def comm_call(body, rows, operand, out_shape, scratch, copies, ident):
    return pl.pallas_call(
        functools.partial(body, rows),
        out_shape=jax.ShapeDtypeStruct(out_shape, F32),
        in_specs=[pl.BlockSpec(memory_space=pltpu.VMEM)],
        out_specs=pl.BlockSpec(memory_space=pl.ANY),
        scratch_shapes=scratch + [pltpu.SemaphoreType.DMA((copies,)), pltpu.SemaphoreType.DMA((copies,)), pltpu.SemaphoreType.DMA],
        compiler_params=pltpu.CompilerParams(collective_id=ident, has_side_effects=True, vmem_limit_bytes=24 * MIB),
        cost_estimate=pl.CostEstimate(flops=rows * 2000, bytes_accessed=80_000_000, transcendentals=0),
    )(operand)


def sum_all(part, ident):
    rows = part.shape[0]
    size = rows // CHUNKS
    scratch = [pltpu.VMEM((CHUNKS, size // 2, BLOCK), F32), pltpu.VMEM((1, rows, BLOCK), F32)] + scatter_scratch(CHUNKS, size) + [pltpu.VMEM((CHUNKS, 6, size // 64, BLOCK), F32)]
    return comm_call(sum_kernel, rows, part, (1, rows, BLOCK), scratch, 22 * CHUNKS, ident)


def stack_planes(part, ident):
    rows = part.shape[0]
    scratch = [pltpu.VMEM((1, rows // 2, BLOCK), F32), pltpu.VMEM((4, rows // 8, BLOCK), F32)] + scatter_scratch(1, rows)
    return comm_call(stack_kernel, rows, part, (4, rows // 8, BLOCK), scratch, 8, ident)


def spread_planes(mine, ident):
    rows = mine.shape[1] * 8
    return comm_call(spread_kernel, rows, mine, (4, rows, BLOCK), [pltpu.VMEM((4, rows, BLOCK), F32)], 10, ident)


def lower_back(up, inv, x_ref, x0, base):
    for k in range(PAIR // PANEL - 1, -1, -1):
        a, b = k * PANEL, (k + 1) * PANEL
        v = base(a, b)
        if b < PAIR:
            v = v - jnp.sum(up[a:b, b:PAIR] * x_ref[0:1, x0 + b:x0 + PAIR], axis=1, keepdims=True)
        x_ref[0:1, x0 + a:x0 + b] = jnp.sum(inv[k] * v, axis=0, keepdims=True)


def fetch_half(planes, stage, sems, first):
    copies = [pltpu.make_async_copy(planes.at[first + i], stage.at[i], sems.at[i]) for i in range(2)]
    for copy in copies:
        copy.start()
    return copies


def fill_half(copies, stage, up, ridge):
    wait_all(copies)
    diag = eye(BLOCK) * ridge
    for i in range(2):
        a, b = i * BLOCK, (i + 1) * BLOCK
        up[a:b, a:b] = stage[i, :BLOCK] + diag
        up[a:b, PAIR:] = stage[i, PAIR:].T


def low_kernel(planes, ridge, up, inv, stage, work, small, sems):
    fill_half(fetch_half(planes, stage, sems, 0), stage, up, ridge[0, 0])
    up[:BLOCK, BLOCK:PAIR] = stage[0, BLOCK:PAIR] + stage[1, BLOCK:PAIR]
    factor(up, inv, work, small, PAIR)


def high_kernel(planes, ridge, up_low, inv_low, cross, design, x_ref, fits, stage, mid, up, inv, work, small, rows, sems):
    copies = fetch_half(planes, stage, sems, 2)
    fetch = pltpu.make_async_copy(design, rows, sems.at[2])
    fetch.start()
    for j in range(2):
        mid[:, j * BLOCK:(j + 1) * BLOCK] = cross[0, j * PAIR:(j + 1) * PAIR, :]
    mid[:, PAIR:] = up_low[:, PAIR:]
    panels = PAIR // PANEL
    for k in range(panels):
        a, b = k * PANEL, (k + 1) * PANEL
        mid[a:b, :PAIR] = dot(inv_low[k], mid[a:b, :PAIR])
        for i in range(k + 1, panels):
            c = i * PANEL
            mid[c:c + PANEL, :PAIR] = mid[c:c + PANEL, :PAIR] - dot(up_low[a:b, c:c + PANEL], mid[a:b, :PAIR], ((0,), (0,)))
    fill_half(copies, stage, up, ridge[0, 0])
    up[:BLOCK, BLOCK:PAIR] = cross[0, 2 * PAIR:2 * PAIR + BLOCK]
    for i in range(panels):
        c = i * PANEL
        up[c:c + PANEL, c:] = up[c:c + PANEL, c:] - dot(mid[:, c:c + PANEL], mid[:, c:], ((0,), (0,)))
    factor(up, inv, work, small, PAIR)
    lower_back(up, inv, x_ref, PAIR, lambda a, b: up[a:b, PAIR:PAIR + 1])
    lower_back(up_low, inv_low, x_ref, 0, lambda a, b: up_low[a:b, PAIR:PAIR + 1] - jnp.sum(
        mid[a:b, :PAIR] * x_ref[0:1, PAIR:], axis=1, keepdims=True))
    fetch.wait()
    z = lax.axis_index('tp')
    x = [x_ref[0:1, pl.ds(pl.multiple_of(z * BLOCK + c * HALF, HALF), HALF)] for c in range(BLOCK // HALF)]
    group = 8

    def fit_rows(g, _):
        lines = []
        for r in range(group):
            base = pl.multiple_of((g * group + r) * HALF, HALF)
            t = sum(rows[pl.ds(base, HALF), c * HALF:(c + 1) * HALF] * x[c] for c in range(BLOCK // HALF))
            lines.append(jnp.sum(t.T, axis=0, keepdims=True))
        fits[pl.ds(pl.multiple_of(g * group, group), group), :] = jnp.concatenate(lines, axis=0)
        return 0

    lax.fori_loop(0, fits.shape[0] // group, fit_rows, 0)


VM = pl.BlockSpec(memory_space=pltpu.VMEM)
SM = pl.BlockSpec(memory_space=pltpu.SMEM)
HB = pl.BlockSpec(memory_space=pl.ANY)
PANELS_SHAPE = (PAIR // PANEL, PANEL, PANEL)


def factor_low(planes, ridge):
    rows = planes.shape[1]
    return pl.pallas_call(
        low_kernel,
        out_shape=(jax.ShapeDtypeStruct((PAIR, PAIR + EXTRA), F32), jax.ShapeDtypeStruct(PANELS_SHAPE, F32)),
        in_specs=[HB, SM],
        out_specs=(VM, VM),
        scratch_shapes=[pltpu.VMEM((2, rows, BLOCK), F32), pltpu.VMEM((HALF, 2 * HALF), F32), pltpu.VMEM((2, HALF, HALF), F32), pltpu.SemaphoreType.DMA((2,))],
        compiler_params=pltpu.CompilerParams(vmem_limit_bytes=24 * MIB),
        cost_estimate=pl.CostEstimate(flops=40_000_000_000, bytes_accessed=10_000_000, transcendentals=0),
        name="factor_low",
    )(planes, ridge)


def factor_high(planes, ridge, up_low, inv_low, cross, design_blk):
    rows = planes.shape[1]
    lines = design_blk.shape[0] // HALF
    return pl.pallas_call(
        high_kernel,
        out_shape=(jax.ShapeDtypeStruct((1, 2 * PAIR), F32), jax.ShapeDtypeStruct((lines, HALF), F32)),
        in_specs=[HB, SM, VM, VM, VM, HB],
        out_specs=(VM, VM),
        scratch_shapes=[
            pltpu.VMEM((2, rows, BLOCK), F32),
            pltpu.VMEM((PAIR, PAIR + EXTRA), F32),
            pltpu.VMEM((PAIR, PAIR + EXTRA), F32),
            pltpu.VMEM(PANELS_SHAPE, F32),
            pltpu.VMEM((HALF, 2 * HALF), F32),
            pltpu.VMEM((2, HALF, HALF), F32),
            pltpu.VMEM(design_blk.shape, F32),
            pltpu.SemaphoreType.DMA((3,)),
        ],
        compiler_params=pltpu.CompilerParams(vmem_limit_bytes=42 * MIB),
        cost_estimate=pl.CostEstimate(flops=50_000_000_000, bytes_accessed=10_000_000, transcendentals=0),
        name="factor_high",
    )(planes, ridge, up_low, inv_low, cross, design_blk)


CROSS_ROWS = 2048


def cross_kernel(early, has_pair, has_prev, own, mate_lo, mate_hi, far_c, far_d, *refs):
    out, panel = refs[-2:]
    z = lax.axis_index('tp')
    mate, even, other = z_peers(z)

    def column(index):
        return pl.ds(pl.multiple_of(index * BLOCK, BLOCK), BLOCK)

    @pl.when(pl.program_id(0) == 0)
    def _():
        out[...] = refs[-3][...] if has_prev else jnp.zeros((CROSS_ROWS, BLOCK), F32)
        if has_pair:
            out[2 * PAIR:2 * PAIR + BLOCK] += refs[0][...]

    full = 1 if early else 0
    panel[:, column(z)] = own[...]
    panel[:, column(even)] = far_d[...]
    panel[:, column(other)] = far_c[...]

    @pl.when(z < 2)
    def _():
        panel[:, column(mate)] = mate_lo[...]

    @pl.when(z >= 2)
    def _():
        panel[:, column(mate)] = mate_hi[...]

    @pl.when((z == full) | (z >= 2))
    def _():
        def row_block(i, _):
            low = panel[:, column(i)]
            for j in range(2):
                a = pl.multiple_of(j * PAIR + i * BLOCK, BLOCK)
                hi = panel[:, PAIR + j * BLOCK:PAIR + (j + 1) * BLOCK]
                out[pl.ds(a, BLOCK)] += dot(low, hi, ((0,), (0,)))
            return 0

        lax.fori_loop(jnp.where(z < 2, 0, full), jnp.where(z < 2, 2, full + 1), row_block, 0)

    if early:
        @pl.when(z >= 2)
        def _():
            out[2 * PAIR:2 * PAIR + BLOCK] += dot(panel[:, PAIR:PAIR + BLOCK], panel[:, PAIR + BLOCK:], ((0,), (0,)))


def cross_gram(early, row0, own, mate_lo, mate_hi, far_c, far_d, prev=None, pair=None):
    rows = far_c.shape[0]
    tile = 256
    steps = rows // tile
    shift = row0 // tile
    near = pl.BlockSpec((tile, BLOCK), lambda i: (i + shift, 0))
    far = pl.BlockSpec((tile, BLOCK), lambda i: (i, 0))
    extras = [a for a in (pair, prev) if a is not None]

    return pl.pallas_call(
        functools.partial(cross_kernel, early, pair is not None, prev is not None),
        out_shape=jax.ShapeDtypeStruct((CROSS_ROWS, BLOCK), F32),
        grid=(steps,),
        in_specs=[near, near, near, far, far] + [pl.BlockSpec(a.shape, lambda i: (0, 0)) for a in extras],
        out_specs=pl.BlockSpec((CROSS_ROWS, BLOCK), lambda i: (0, 0)),
        scratch_shapes=[pltpu.VMEM((tile, 2 * PAIR), F32)],
        compiler_params=pltpu.CompilerParams(dimension_semantics=("arbitrary",), vmem_limit_bytes=24 * MIB),
        cost_estimate=pl.CostEstimate(flops=rows * 6_000_000, bytes_accessed=rows * 8000, transcendentals=0),
        name="cross_gram",
    )(own, mate_lo, mate_hi, far_c, far_d, *extras)


def pair_kernel(low, count, *refs):
    nears, mates, heads, out = refs[:count], refs[count:2 * count], refs[2 * count:-1], refs[-1]
    z = lax.axis_index('tp')
    r = BLOCK if low else 0

    @pl.when(pl.program_id(0) == 0)
    def _():
        if len(heads) == 1:
            out[...] = heads[0][...]
        elif low:
            out[:BLOCK] = heads[0][...]
            out[BLOCK:PAIR] = jnp.zeros((BLOCK, BLOCK), F32)
            out[PAIR:] = jnp.broadcast_to(heads[1][...], (EXTRA, BLOCK))
        else:
            out[...] = jnp.zeros((BLOCK, BLOCK), F32)

    mine = z < 2 if low else z >= 2
    for odd in range(2):
        @pl.when(mine & (lax.rem(z, 2) == odd))
        def _():
            for near, mate in zip(nears, mates):
                one, two = (mate, near) if odd else (near, mate)
                out[r:r + BLOCK] += dot(one[...], two[...], ((0,), (0,)))


def pair_gram(low, nears, mates, heads, row0=0):
    rows = mates[0].shape[0]
    tile = 256
    out_rows = PAIR + EXTRA if low else BLOCK
    shift = row0 // tile
    near = pl.BlockSpec((tile, BLOCK), lambda i: (i + shift, 0))
    far = pl.BlockSpec((tile, BLOCK), lambda i: (i, 0))
    return pl.pallas_call(
        functools.partial(pair_kernel, low, len(nears)),
        out_shape=jax.ShapeDtypeStruct((out_rows, BLOCK), F32),
        grid=(rows // tile,),
        in_specs=[near] * len(nears) + [far] * len(nears) + [pl.BlockSpec(h.shape, lambda i: (0, 0)) for h in heads],
        out_specs=pl.BlockSpec((out_rows, BLOCK), lambda i: (0, 0)),
        compiler_params=pltpu.CompilerParams(dimension_semantics=("arbitrary",), vmem_limit_bytes=24 * MIB),
        cost_estimate=pl.CostEstimate(flops=rows * 3_000_000 * len(nears), bytes_accessed=rows * 6000, transcendentals=0),
        name="pair_gram",
    )(*nears, *mates, *heads)


def residual_kernel(fit, target, out, got, send_sem, recv_sem):
    z, dp = lax.axis_index('tp'), lax.axis_index('dp')
    peers = [{'tp': p, 'dp': dp} for p in z_peers(z)]
    meet(peers)
    start = starter(send_sem, recv_sem)
    wait_all([start(fit, got.at[j], peer) for j, peer in enumerate(peers)])
    out[...] = target[...] - ((fit[...] + got[0]) + (got[1] + got[2]))


def residual(fits, target_tile):
    return pl.pallas_call(
        residual_kernel,
        out_shape=jax.ShapeDtypeStruct(target_tile.shape, F32),
        in_specs=[VM, VM],
        out_specs=VM,
        scratch_shapes=[pltpu.VMEM((3,) + target_tile.shape, F32), pltpu.SemaphoreType.DMA((3,)), pltpu.SemaphoreType.DMA((3,))],
        compiler_params=pltpu.CompilerParams(collective_id=3, has_side_effects=True),
        cost_estimate=pl.CostEstimate(flops=3_000_000_000, bytes_accessed=1_000_000, transcendentals=0),
        name="residual",
    )(fits, target_tile)


EDGES = (0, 512, 1536, 2048)


def solution(mesh):
    col_ways, row_ways = mesh.shape['tp'], mesh.shape['dp']

    def swap(block, one, two):
        pairs = [(s * row_ways + d, t * row_ways + d) for s, t in ((one, two), (two, one)) for d in range(row_ways)]
        return lax.ppermute(block, ('tp', 'dp'), pairs)

    def local_fit(design_blk, target_blk, ridge):
        rows_dev, _ = design_blk.shape
        quarter_rows = rows_dev // col_ways
        z = lax.axis_index('tp')

        def piece(array, index):
            return lax.dynamic_slice_in_dim(array, index * quarter_rows, quarter_rows)

        to_mate = piece(design_blk, z ^ 1)
        to_mate, design_b = lax.optimization_barrier((to_mate, design_blk))
        low_a = swap(to_mate, 0, 1)
        to_third = piece(design_b, z ^ 3)
        to_third, design_b = lax.optimization_barrier((to_third, design_b))
        to_even = piece(design_b, z ^ 2)
        low_b = swap(to_third, 0, 1)
        near_c = swap(to_third, 1, 2)
        near_d = swap(to_even, 1, 3)
        high_a = swap(to_mate, 2, 3)
        to_third_b, to_even_b, design_b = lax.optimization_barrier((to_third, to_even, design_b))
        own = piece(design_b, z)
        chunks = [(to_third_b[i:j], to_even_b[i:j]) for i, j in zip(EDGES, EDGES[1:])]
        late_b = to_third_b[EDGES[1]:]
        own_gram = dot(design_b, design_b, ((0,), (0,)))
        moment = dot(target_blk[None, :], design_b)
        part = pair_gram(True, (own,), (low_a,), (own_gram, moment))
        low_a, low_b, near_c, near_d, part, chunks = lax.optimization_barrier(
            (low_a, low_b, near_c, near_d, part, chunks))
        far_c, far_d = [], []

        def send_late(pieces):
            far_c.append(swap(pieces[0], 0, 3))
            far_d.append(swap(pieces[1], 0, 2))

        send_late(chunks[0])
        high_b0 = swap(chunks[0][0], 2, 3)
        part = pair_gram(True, (to_even,), (low_b,), (part,))
        mine = stack_planes(part, 1)
        mine, late_b, chunks = lax.optimization_barrier((mine, late_b, chunks))
        send_late(chunks[1])
        high_b1 = swap(late_b, 2, 3)
        send_late(chunks[2])
        planes = spread_planes(mine, 2)
        ridge_cell = jnp.reshape(ridge, (1, 1))
        up_low, inv_low = factor_low(planes, ridge_cell)
        own_b, near_c, up_low = lax.optimization_barrier((own, near_c, up_low))
        cross = cross_gram(True, 0, own_b, low_a, high_a, near_c, near_d)
        cross = cross_gram(False, EDGES[0], own_b, low_a, high_a, far_c[0], far_d[0], cross)
        pair_high = pair_gram(False, (to_even,), (high_b0,), ())
        cross = cross_gram(False, EDGES[1], own_b, low_a, high_a, far_c[1], far_d[1], cross)
        high_b1, cross = lax.optimization_barrier((high_b1, cross))
        pair_high = pair_gram(False, (to_even,), (high_b1,), (pair_high,), EDGES[1])
        cross = cross_gram(False, EDGES[2], own_b, low_a, high_a, far_c[2], far_d[2], cross, pair_high)
        cross = sum_all(cross, 4)
        x_row, fits = factor_high(planes, ridge_cell, up_low, inv_low, cross, design_b)
        left = residual(fits, jnp.reshape(target_blk, (rows_dev // HALF, HALF)))
        return x_row[0], jnp.reshape(left, (rows_dev,))

    return jax.shard_map(local_fit, mesh=mesh, in_specs=(P('dp', 'tp'), P('dp'), P()), out_specs=(P(), P('dp')), check_vma=False)
```

profile of v0, /device:TPU:0, one launch (start us, length us, event | category | flops | bytes accessed | tf_op | source)
XLA Modules:
  0.0 487.9 jit_solution(12218425206754993273)
XLA Ops:
  0.6 3.8 constant_dynamic-slice_fusion.3
  4.5 4.9 %collective-permute-start = (f32[2048,384]{1,0:T(8,128)}, f32[2048,384]{1,0:T(8,128)}, u32[]{:S(2)}, u32[]{:S(2)}) collective-permute-start(f32[2048,384]{1,0:T(8,128)} %constant_dynamic-slice_fusion.3), channel_id=1, source_target_pairs={{0,8},{1,9},{2,10},{3,11},{4,12},{5,13},{6,14},{7,15},{8,0},{9,1},... | collective-permute-start | bytes 9437192 | tf_op jit(solution)/shard_map/ppermute | solution.py:570
  37.4 9.9 %fusion.3.refs_3_ = f32[1,384]{1,0:T(1,128)S(1)} fusion(f32[8192,384]{1,0:T(8,128)} %design, f32[8192,1]{0,1:T(1,128)S(1)} %bitcast.13), kind=kOutput, calls=%fused_computation.7 | convolution fusion | flops 37748736 | bytes 12617216 | tf_op jit(solution)/shard_map/dot_general | solution.py:18
  47.3 20.4 %fusion.2.refs_2_ = f32[384,384]{1,0:T(8,128)S(1)} fusion(f32[8192,384]{1,0:T(8,128)S(1)} %bitcast.11), kind=kOutput, calls=%fused_computation.6 | convolution fusion | flops 14495514624 | bytes 13172736 | tf_op jit(solution)/shard_map/dot_general | solution.py:18
  67.7 11.0 %collective-permute-done.refs_1_.mate_lo = f32[2048,384]{1,0:T(8,128)} collective-permute-done((f32[2048,384]{1,0:T(8,128)}, f32[2048,384]{1,0:T(8,128)}, u32[]{:S(2)}, u32[]{:S(2)}) %collective-permute-start) | collective-permute-done | bytes 3145760 | tf_op jit(solution)/shard_map/ppermute | solution.py:570
  78.7 8.4 %pair_gram.4.refs_2_ = f32[896,384]{1,0:T(8,128)S(1)} custom-call(f32[2048,384]{1,0:T(8,128)S(1)} %constant_dynamic-slice_fusion.refs_0_.own, f32[2048,384]{1,0:T(8,128)} %collective-permute-done.refs_1_.mate_lo, f32[384,384]{1,0:T(8,128)S(1)} %fusion.2.refs_2_, f32[1,384]{1,0:T(1,128)S(1)} %fusion.3.refs_3_), custom_call_target="tpu_custom_call" | custom-call | flops 6144000000 | bytes 12288000 | tf_op jit(solution)/shard_map/pair_gram/pallas_call | solution.py:528
  87.1 58.1 %collective-permute-done.1.refs_1_ = f32[2048,384]{1,0:T(8,128)} collective-permute-done((f32[2048,384]{1,0:T(8,128)}, f32[2048,384]{1,0:T(8,128)}, u32[]{:S(2)}, u32[]{:S(2)}) %collective-permute-start.1) | collective-permute-done | bytes 3145760 | tf_op jit(solution)/shard_map/ppermute | solution.py:570
  145.2 14.6 %collective-permute-start.10 = (f32[512,384]{1,0:T(8,128)}, f32[512,384]{1,0:T(8,128)S(1)}, u32[]{:S(2)}, u32[]{:S(2)}) collective-permute-start(f32[512,384]{1,0:T(8,128)} %get-tuple-element.44), channel_id=1, source_target_pairs={{0,24},{1,25},{2,26},{3,27},{4,28},{5,29},{6,30},{7,31},{24,0},{25... | collective-permute-start | bytes 2359304 | tf_op jit(solution)/shard_map/ppermute | solution.py:570
  160.6 8.5 %pair_gram.5.part = f32[896,384]{1,0:T(8,128)S(1)} custom-call(f32[2048,384]{1,0:T(8,128)S(1)} %constant_dynamic-slice_fusion.1.refs_0_, f32[2048,384]{1,0:T(8,128)} %collective-permute-done.1.refs_1_, f32[896,384]{1,0:T(8,128)S(1)} %pair_gram.4.refs_2_), custom_call_target="tpu_custom_call" | custom-call | flops 6144000000 | bytes 12288000 | tf_op jit(solution)/shard_map/pair_gram/pallas_call | solution.py:528
  169.2 35.3 %shard_map.50.mine = f32[4,112,384]{2,1,0:T(8,128)S(1)} custom-call(f32[896,384]{1,0:T(8,128)S(1)} %pair_gram.5.part), custom_call_target="tpu_custom_call" | custom-call | flops 1792000 | bytes 80000000 | tf_op jit(solution)/shard_map/pallas_call | solution.py:282
  208.1 28.8 %shard_map.51.planes = f32[4,896,384]{2,1,0:T(8,128)S(1)} custom-call(f32[4,112,384]{2,1,0:T(8,128)S(1)} %shard_map.50.mine), custom_call_target="tpu_custom_call" | custom-call | flops 1792000 | bytes 80000000 | tf_op jit(solution)/shard_map/pallas_call | solution.py:282
  237.8 27.7 %factor_low.1 = (f32[768,896]{1,0:T(8,128)S(1)}, f32[3,256,256]{2,1,0:T(8,128)S(1)}) custom-call(f32[4,896,384]{2,1,0:T(8,128)S(1)} %shard_map.51.planes, f32[1,1]{1,0:T(1,128)} %bitcast.8.ridge), custom_call_target="tpu_custom_call" | custom-call | flops 40000000000 | bytes 10000000 | tf_op jit(solution)/shard_map/factor_low/pallas_call | solution.py:390
  267.1 5.3 %collective-permute-start.8 = (f32[1024,384]{1,0:T(8,128)}, f32[1024,384]{1,0:T(8,128)S(1)}, u32[]{:S(2)}, u32[]{:S(2)}) collective-permute-start(f32[1024,384]{1,0:T(8,128)} %slice.23), channel_id=1, source_target_pairs={{0,24},{1,25},{2,26},{3,27},{4,28},{5,29},{6,30},{7,31},{24,0},{25... | collective-permute-start | bytes 4718600 | tf_op jit(solution)/shard_map/ppermute | solution.py:570
  274.3 7.1 %cross_gram.4.refs_0_ = f32[2048,384]{1,0:T(8,128)S(1)} custom-call(f32[2048,384]{1,0:T(8,128)S(1)} %constant_dynamic-slice_fusion.refs_0_.own, f32[2048,384]{1,0:T(8,128)} %collective-permute-done.refs_1_.mate_lo, f32[2048,384]{1,0:T(8,128)} %collective-permute-done.4.mate_hi, f32[2048,384]{1,0:T(8,128)} %collective-permute-done.2.far_c, ...), custom_call_target="tpu_custom_call" | custom-call | flops 12288000000 | bytes 16384000 | tf_op jit(solution)/shard_map/cross_gram/pallas_call | solution.py:483
  282.6 16.1 %collective-permute-start.5 = (f32[512,384]{1,0:T(8,128)S(1)}, f32[512,384]{1,0:T(8,128)S(1)}, u32[]{:S(2)}, u32[]{:S(2)}) collective-permute-start(f32[512,384]{1,0:T(8,128)S(1)} %copy-done.6), channel_id=1, source_target_pairs={{0,24},{1,25},{2,26},{3,27},{4,28},{5,29},{6,30},{7,31},{24,0},{25... | collective-permute-start | bytes 2359304 | tf_op jit(solution)/shard_map/ppermute | solution.py:570
  298.7 4.4 collective-permute-start.6
  303.1 7.4 %cross_gram.5.refs_0_ = f32[2048,384]{1,0:T(8,128)S(1)} custom-call(f32[2048,384]{1,0:T(8,128)S(1)} %constant_dynamic-slice_fusion.refs_0_.own, f32[2048,384]{1,0:T(8,128)} %collective-permute-done.refs_1_.mate_lo, f32[2048,384]{1,0:T(8,128)} %collective-permute-done.4.mate_hi, f32[512,384]{1,0:T(8,128)S(1)} %collective-permute-done.10.far_c, ...), custom_call_target="tpu_custom_call" | custom-call | flops 3072000000 | bytes 4096000 | tf_op jit(solution)/shard_map/cross_gram/pallas_call | solution.py:483
  310.4 16.7 %collective-permute-done.8.far_c = f32[1024,384]{1,0:T(8,128)S(1)} collective-permute-done((f32[1024,384]{1,0:T(8,128)}, f32[1024,384]{1,0:T(8,128)S(1)}, u32[]{:S(2)}, u32[]{:S(2)}) %collective-permute-start.8) | collective-permute-done | bytes 1572896 | tf_op jit(solution)/shard_map/ppermute | solution.py:570
  327.1 36.1 %collective-permute-done.9.far_d = f32[1024,384]{1,0:T(8,128)S(1)} collective-permute-done((f32[1024,384]{1,0:T(8,128)}, f32[1024,384]{1,0:T(8,128)S(1)}, u32[]{:S(2)}, u32[]{:S(2)}) %collective-permute-start.9) | collective-permute-done | bytes 1572896 | tf_op jit(solution)/shard_map/ppermute | solution.py:570
  363.2 13.6 %cross_gram.6.refs_1_ = f32[2048,384]{1,0:T(8,128)S(1)} custom-call(f32[2048,384]{1,0:T(8,128)S(1)} %constant_dynamic-slice_fusion.refs_0_.own, f32[2048,384]{1,0:T(8,128)} %collective-permute-done.refs_1_.mate_lo, f32[2048,384]{1,0:T(8,128)} %collective-permute-done.4.mate_hi, f32[1024,384]{1,0:T(8,128)S(1)} %collective-permute-done.8.far_c, ...), custom_call_target="tpu_custom_call" | custom-call | flops 6144000000 | bytes 8192000 | tf_op jit(solution)/shard_map/cross_gram/pallas_call | solution.py:483
  378.9 7.4 %cross_gram.7.part = f32[2048,384]{1,0:T(8,128)S(1)} custom-call(f32[2048,384]{1,0:T(8,128)S(1)} %constant_dynamic-slice_fusion.refs_0_.own, f32[2048,384]{1,0:T(8,128)} %collective-permute-done.refs_1_.mate_lo, f32[2048,384]{1,0:T(8,128)} %collective-permute-done.4.mate_hi, f32[512,384]{1,0:T(8,128)S(1)} %collective-permute-done.5.far_c, ...), custom_call_target="tpu_custom_call" | custom-call | flops 3072000000 | bytes 4096000 | tf_op jit(solution)/shard_map/cross_gram/pallas_call | solution.py:483
  386.4 48.4 %shard_map.52.cross = f32[1,2048,384]{2,1,0:T(8,128)S(1)} custom-call(f32[2048,384]{1,0:T(8,128)S(1)} %cross_gram.7.part), custom_call_target="tpu_custom_call" | custom-call | flops 4096000 | bytes 80000000 | tf_op jit(solution)/shard_map/pallas_call | solution.py:282
  434.8 42.0 %factor_high.1 = (f32[1,1536]{1,0:T(1,128)S(1)}, f32[64,128]{1,0:T(8,128)S(1)}) custom-call(f32[4,896,384]{2,1,0:T(8,128)S(1)} %shard_map.51.planes, f32[1,1]{1,0:T(1,128)} %bitcast.9.ridge, f32[768,896]{1,0:T(8,128)S(1)} %copy-done.2, f32[3,256,256]{2,1,0:T(8,128)S(1)} %copy-done.4, f32[1,2048,384]{2,1,0:T(8,128)S(1)} %shard_map.52.cross, f32[8192,384]{1,0:T(8,128)} %design), custom_call_target="tpu_custom_call" | custom-call | flops 49999998976 | bytes 10000000 | tf_op jit(solution)/shard_map/factor_high/pallas_call | solution.py:405
  477.4 8.3 %residual.1 = f32[64,128]{1,0:T(8,128)} custom-call(f32[64,128]{1,0:T(8,128)} %copy-done, f32[64,128]{1,0:T(8,128)} %bitcast.12), custom_call_target="tpu_custom_call" | custom-call | flops 3000000000 | bytes 1000000 | tf_op jit(solution)/shard_map/residual/pallas_call | solution.py:550
  (51 shorter events, 41.6 us)
Async XLA Ops:
  4.5 74.2 %collective-permute-start = (f32[2048,384]{1,0:T(8,128)}, f32[2048,384]{1,0:T(8,128)}, u32[]{:S(2)}, u32[]{:S(2)}) collective-permute-start(f32[2048,384]{1,0:T(8,128)} %constant_dynamic-slice_fusion.3), channel_id=1, source_target_pairs={{0,8},{1,9},{2,10},{3,11},{4,12},{5,13},{6,14},{7,15},{8,0},{9,1},... | collective-permute-start | bytes 9437192 | tf_op jit(solution)/shard_map/ppermute | solution.py:570
  13.2 132.1 %collective-permute-start.1 = (f32[2048,384]{1,0:T(8,128)}, f32[2048,384]{1,0:T(8,128)}, u32[]{:S(2)}, u32[]{:S(2)}) collective-permute-start(f32[2048,384]{1,0:T(8,128)} %constant_dynamic-slice_fusion.2), channel_id=1, source_target_pairs={{0,8},{1,9},{2,10},{3,11},{4,12},{5,13},{6,14},{7,15},{8,0},{9,1},... | collective-permute-start | bytes 9437192 | tf_op jit(solution)/shard_map/ppermute | solution.py:570
  15.1 130.2 %collective-permute-start.2 = (f32[2048,384]{1,0:T(8,128)}, f32[2048,384]{1,0:T(8,128)}, u32[]{:S(2)}, u32[]{:S(2)}) collective-permute-start(f32[2048,384]{1,0:T(8,128)} %constant_dynamic-slice_fusion.2), channel_id=1, source_target_pairs={{8,16},{9,17},{10,18},{11,19},{12,20},{13,21},{14,22},{15,23},{16,... | collective-permute-start | bytes 9437192 | tf_op jit(solution)/shard_map/ppermute | solution.py:570
  17.4 249.7 %collective-permute-start.4 = (f32[2048,384]{1,0:T(8,128)}, f32[2048,384]{1,0:T(8,128)}, u32[]{:S(2)}, u32[]{:S(2)}) collective-permute-start(f32[2048,384]{1,0:T(8,128)} %constant_dynamic-slice_fusion.3), channel_id=1, source_target_pairs={{16,24},{17,25},{18,26},{19,27},{20,28},{21,29},{22,30},{23,31},{2... | collective-permute-start | bytes 9437192 | tf_op jit(solution)/shard_map/ppermute | solution.py:570
  21.8 65.3 %collective-permute-start.3 = (f32[2048,384]{1,0:T(8,128)S(1)}, f32[2048,384]{1,0:T(8,128)}, u32[]{:S(2)}, u32[]{:S(2)}) collective-permute-start(f32[2048,384]{1,0:T(8,128)S(1)} %constant_dynamic-slice_fusion.1.refs_0_), channel_id=1, source_target_pairs={{8,24},{9,25},{10,26},{11,27},{12,28},{13,29},{14,30},{15,31},{24,... | collective-permute-start | bytes 9437192 | tf_op jit(solution)/shard_map/ppermute | solution.py:570
  32.0 15.2 %slice-start = ((s8[12582912]{0:T(1024)(128)(4,1)}), s8[4194304]{0:T(1024)(128)(4,1)S(1)}, s32[]{:S(2)}) async-start(s8[12582912]{0:T(1024)(128)(4,1)} %bitcast.10), calls=%async_computation | async-start | bytes 8388608
  34.3 3.1 copy-start.7
  34.3 13.0 %slice-start.1 = ((s8[12582912]{0:T(1024)(128)(4,1)}), s8[4194304]{0:T(1024)(128)(4,1)S(1)}, s32[]{:S(2)}) async-start(s8[12582912]{0:T(1024)(128)(4,1)} %bitcast.10), calls=%async_computation.1 | async-start | bytes 8388608
  37.4 9.9 %slice-start.2 = ((s8[12582912]{0:T(1024)(128)(4,1)}), s8[4194304]{0:T(1024)(128)(4,1)S(1)}, s32[]{:S(2)}) async-start(s8[12582912]{0:T(1024)(128)(4,1)} %bitcast.10), calls=%async_computation.2 | async-start | bytes 8388608
  145.2 136.4 %collective-permute-start.10 = (f32[512,384]{1,0:T(8,128)}, f32[512,384]{1,0:T(8,128)S(1)}, u32[]{:S(2)}, u32[]{:S(2)}) collective-permute-start(f32[512,384]{1,0:T(8,128)} %get-tuple-element.44), channel_id=1, source_target_pairs={{0,24},{1,25},{2,26},{3,27},{4,28},{5,29},{6,30},{7,31},{24,0},{25... | collective-permute-start | bytes 2359304 | tf_op jit(solution)/shard_map/ppermute | solution.py:570
  159.9 112.5 %collective-permute-start.12 = (f32[512,384]{1,0:T(8,128)}, f32[512,384]{1,0:T(8,128)S(1)}, u32[]{:S(2)}, u32[]{:S(2)}) collective-permute-start(f32[512,384]{1,0:T(8,128)} %get-tuple-element.44), channel_id=1, source_target_pairs={{16,24},{17,25},{18,26},{19,27},{20,28},{21,29},{22,30},{23,31},{2... | collective-permute-start | bytes 2359304 | tf_op jit(solution)/shard_map/ppermute | solution.py:570
  204.5 32.5 %copy-start.5 = (f32[1536,384]{1,0:T(8,128)S(1)}, f32[1536,384]{1,0:T(8,128)}, u32[]{:S(2)}) copy-start(f32[1536,384]{1,0:T(8,128)} %slice.27) | copy-start | bytes 7077892
  204.5 94.2 %collective-permute-start.11 = (f32[512,384]{1,0:T(8,128)}, f32[512,384]{1,0:T(8,128)S(1)}, u32[]{:S(2)}, u32[]{:S(2)}) collective-permute-start(f32[512,384]{1,0:T(8,128)} %get-tuple-element.45), channel_id=1, source_target_pairs={{0,16},{1,17},{2,18},{3,19},{4,20},{5,21},{6,22},{7,23},{16,0},{17... | collective-permute-start | bytes 2359304 | tf_op jit(solution)/shard_map/ppermute | solution.py:570
  237.0 139.9 %collective-permute-start.7 = (f32[1536,384]{1,0:T(8,128)S(1)}, f32[1536,384]{1,0:T(8,128)S(1)}, u32[]{:S(2)}, u32[]{:S(2)}) collective-permute-start(f32[1536,384]{1,0:T(8,128)S(1)} %copy-done.5), channel_id=1, source_target_pairs={{16,24},{17,25},{18,26},{19,27},{20,28},{21,29},{22,30},{23,31},{2... | collective-permute-start | bytes 7077896 | tf_op jit(solution)/shard_map/ppermute | solution.py:570
  265.6 1.5 copy-start.1
  267.1 14.4 %copy-start.3 = (f32[3,256,256]{2,1,0:T(8,128)}, f32[3,256,256]{2,1,0:T(8,128)S(1)}, u32[]{:S(2)}) copy-start(f32[3,256,256]{2,1,0:T(8,128)S(1)} %get-tuple-element.54.inv_low) | copy-start | bytes 2359300
  267.1 60.0 %collective-permute-start.8 = (f32[1024,384]{1,0:T(8,128)}, f32[1024,384]{1,0:T(8,128)S(1)}, u32[]{:S(2)}, u32[]{:S(2)}) collective-permute-start(f32[1024,384]{1,0:T(8,128)} %slice.23), channel_id=1, source_target_pairs={{0,24},{1,25},{2,26},{3,27},{4,28},{5,29},{6,30},{7,31},{24,0},{25... | collective-permute-start | bytes 4718600 | tf_op jit(solution)/shard_map/ppermute | solution.py:570
  272.4 90.8 %collective-permute-start.9 = (f32[1024,384]{1,0:T(8,128)}, f32[1024,384]{1,0:T(8,128)S(1)}, u32[]{:S(2)}, u32[]{:S(2)}) collective-permute-start(f32[1024,384]{1,0:T(8,128)} %slice.24), channel_id=1, source_target_pairs={{0,16},{1,17},{2,18},{3,19},{4,20},{5,21},{6,22},{7,23},{16,0},{17... | collective-permute-start | bytes 4718600 | tf_op jit(solution)/shard_map/ppermute | solution.py:570
  281.5 1.1 copy-start.6
  282.6 94.5 %collective-permute-start.5 = (f32[512,384]{1,0:T(8,128)S(1)}, f32[512,384]{1,0:T(8,128)S(1)}, u32[]{:S(2)}, u32[]{:S(2)}) collective-permute-start(f32[512,384]{1,0:T(8,128)S(1)} %copy-done.6), channel_id=1, source_target_pairs={{0,24},{1,25},{2,26},{3,27},{4,28},{5,29},{6,30},{7,31},{24,0},{25... | collective-permute-start | bytes 2359304 | tf_op jit(solution)/shard_map/ppermute | solution.py:570
  298.7 80.3 %collective-permute-start.6 = (f32[512,384]{1,0:T(8,128)S(1)}, f32[512,384]{1,0:T(8,128)S(1)}, u32[]{:S(2)}, u32[]{:S(2)}) collective-permute-start(f32[512,384]{1,0:T(8,128)S(1)} %get-tuple-element.58), channel_id=1, source_target_pairs={{0,16},{1,17},{2,18},{3,19},{4,20},{5,21},{6,22},{7,23},{16,0},{17... | collective-permute-start | bytes 2359304 | tf_op jit(solution)/shard_map/ppermute | solution.py:570
  386.4 48.5 %copy-start.2 = (f32[768,896]{1,0:T(8,128)S(1)}, f32[768,896]{1,0:T(8,128)}, u32[]{:S(2)}) copy-start(f32[768,896]{1,0:T(8,128)} %copy-done.1) | copy-start | bytes 8257540
  386.4 48.5 %copy-start.4 = (f32[3,256,256]{2,1,0:T(8,128)S(1)}, f32[3,256,256]{2,1,0:T(8,128)}, u32[]{:S(2)}) copy-start(f32[3,256,256]{2,1,0:T(8,128)} %copy-done.3) | copy-start | bytes 2359300
  476.8 0.6 copy-start
where the time goes:
time: 493 us; the launch traced here: 488 us
  Pallas kernels  243 us (49%)
  waiting for transfers between devices  124 us (25%)
  starting transfers between devices  61.3 us (12%)
  matrix products  30.3 us (6%)
  local copies, waits for them, and re-layouts  26.7 us (5%)
    ppermute x13, waiting for transfers between devices, swap(): return lax.ppermute(block, ('tp', 'dp'), pairs)  124 us
    pallas_call x3, Pallas kernels, comm_call(): pl.pallas_call(functools.partial(body, rows), out_shape=jax.ShapeDtypeStr...  113 us
    ppermute x13, starting transfers between devices, swap(): return lax.ppermute(block, ('tp', 'dp'), pairs)  61.3 us
    pallas_call x1, Pallas kernels, factor_high(): pl.pallas_call(high_kernel, out_shape=(jax.ShapeDtypeStruct((1, 2 * PAIR)...  42 us
    pallas_call x4, Pallas kernels, cross_gram(): pl.pallas_call(functools.partial(cross_kernel, early, pair is not None, p...  35.5 us
    dot_general x2, matrix products, dot(): lax.dot_general(a, b, (dims, ((), ())), precision=HIGHEST, preferred_elem...  30.3 us
    pallas_call x1, Pallas kernels, factor_low(): pl.pallas_call(low_kernel, out_shape=(jax.ShapeDtypeStruct((PAIR, PAIR +...  27.7 us
    pallas_call x4, Pallas kernels, pair_gram(): pl.pallas_call(functools.partial(pair_kernel, low, len(nears)), out_shape...  17.3 us
  transfers between devices with their start and end apart: 13, of which 5 were waited for; matrix products, arithmetic and copies ran while one was open for 10% of the time, Pallas kernels for 28%

commit v1 on v0

--- a/solution.py
+++ b/solution.py
@@ -268,7 +268,7 @@
     full[:, at(own + a2, sixt)] = mine[:, :sixt]
     full[:, at(own + b2, sixt)] = mine[:, sixt:]
     start = starter(send_sem, recv_sem)
-    in_turn(plane_gather(rows, full.at[2 * c:2 * c + 2], start, peers, where) for c in range(2))
+    in_turn(plane_gather(rows, full.at[c:c + 1], start, peers, where) for c in range(4))
     copy = pltpu.make_async_copy(full, out, out_sem)
     copy.start()
     copy.wait()
@@ -305,7 +305,7 @@
 
 def spread_planes(mine, ident):
     rows = mine.shape[1] * 8
-    return comm_call(spread_kernel, rows, mine, (4, rows, BLOCK), [pltpu.VMEM((4, rows, BLOCK), F32)], 10, ident)
+    return comm_call(spread_kernel, rows, mine, (4, rows, BLOCK), [pltpu.VMEM((4, rows, BLOCK), F32)], 20, ident)
 
 
 def lower_back(up, inv, x_ref, x0, base):
@@ -493,48 +493,66 @@
     )(own, mate_lo, mate_hi, far_c, far_d, *extras)
 
 
-def pair_kernel(low, count, *refs):
-    nears, mates, heads, out = refs[:count], refs[count:2 * count], refs[2 * count:-1], refs[-1]
+def own_kernel(design, target, part):
+    @pl.when(pl.program_id(0) == 0)
+    def _():
+        part[...] = jnp.zeros_like(part)
+
+    part[:BLOCK] += dot(design[...], design[...], ((0,), (0,)))
+    part[PAIR:PAIR + 1] += dot(target[0], design[...])
+
+
+def own_gram(design_blk, target_blk):
+    rows = design_blk.shape[0]
+    tile = 256
+    return pl.pallas_call(
+        own_kernel,
+        out_shape=jax.ShapeDtypeStruct((PAIR + EXTRA, BLOCK), F32),
+        grid=(rows // tile,),
+        in_specs=[pl.BlockSpec((tile, BLOCK), lambda i: (i, 0)), pl.BlockSpec((1, 1, tile), lambda i: (i, 0, 0))],
+        out_specs=pl.BlockSpec((PAIR + EXTRA, BLOCK), lambda i: (0, 0)),
+        compiler_params=pltpu.CompilerParams(dimension_semantics=("arbitrary",), vmem_limit_bytes=24 * MIB),
+        cost_estimate=pl.CostEstimate(flops=30_000_000_000, bytes_accessed=13_000_000, transcendentals=0),
+        name="own_gram",
+    )(design_blk, jnp.reshape(target_blk, (rows // tile, 1, tile)))
+
+
+def pair_kernel(low, near, mate, head, out, panel):
     z = lax.axis_index('tp')
     r = BLOCK if low else 0
 
     @pl.when(pl.program_id(0) == 0)
     def _():
-        if len(heads) == 1:
-            out[...] = heads[0][...]
-        elif low:
-            out[:BLOCK] = heads[0][...]
-            out[BLOCK:PAIR] = jnp.zeros((BLOCK, BLOCK), F32)
-            out[PAIR:] = jnp.broadcast_to(heads[1][...], (EXTRA, BLOCK))
-        else:
-            out[...] = jnp.zeros((BLOCK, BLOCK), F32)
-
-    mine = z < 2 if low else z >= 2
-    for odd in range(2):
-        @pl.when(mine & (lax.rem(z, 2) == odd))
-        def _():
-            for near, mate in zip(nears, mates):
-                one, two = (mate, near) if odd else (near, mate)
-                out[r:r + BLOCK] += dot(one[...], two[...], ((0,), (0,)))
-
-
-def pair_gram(low, nears, mates, heads, row0=0):
-    rows = mates[0].shape[0]
+        out[...] = head[...] if out.shape == head.shape else jnp.zeros_like(out)
+
+    @pl.when(z < 2 if low else z >= 2)
+    def _():
+        odd = lax.rem(z, 2)
+        panel[:, pl.ds(pl.multiple_of(odd * BLOCK, BLOCK), BLOCK)] = near[...]
+        panel[:, pl.ds(pl.multiple_of((1 - odd) * BLOCK, BLOCK), BLOCK)] = mate[...]
+        out[r:r + BLOCK] += dot(panel[:, :BLOCK], panel[:, BLOCK:], ((0,), (0,)))
+
+
+def pair_gram(low, near_rows, mate, head, row0=0):
+    rows = mate.shape[0]
     tile = 256
+    shift = row0 // tile
     out_rows = PAIR + EXTRA if low else BLOCK
-    shift = row0 // tile
-    near = pl.BlockSpec((tile, BLOCK), lambda i: (i + shift, 0))
-    far = pl.BlockSpec((tile, BLOCK), lambda i: (i, 0))
     return pl.pallas_call(
-        functools.partial(pair_kernel, low, len(nears)),
+        functools.partial(pair_kernel, low),
         out_shape=jax.ShapeDtypeStruct((out_rows, BLOCK), F32),
         grid=(rows // tile,),
-        in_specs=[near] * len(nears) + [far] * len(nears) + [pl.BlockSpec(h.shape, lambda i: (0, 0)) for h in heads],
+        in_specs=[
+            pl.BlockSpec((tile, BLOCK), lambda i: (i + shift, 0)),
+            pl.BlockSpec((tile, BLOCK), lambda i: (i, 0)),
+            pl.BlockSpec(head.shape, lambda i: (0, 0)),
+        ],
         out_specs=pl.BlockSpec((out_rows, BLOCK), lambda i: (0, 0)),
+        scratch_shapes=[pltpu.VMEM((tile, PAIR), F32)],
         compiler_params=pltpu.CompilerParams(dimension_semantics=("arbitrary",), vmem_limit_bytes=24 * MIB),
-        cost_estimate=pl.CostEstimate(flops=rows * 3_000_000 * len(nears), bytes_accessed=rows * 6000, transcendentals=0),
+        cost_estimate=pl.CostEstimate(flops=rows * 3_000_000, bytes_accessed=rows * 6000, transcendentals=0),
         name="pair_gram",
-    )(*nears, *mates, *heads)
+    )(near_rows, mate, head)
 
 
 def residual_kernel(fit, target, out, got, send_sem, recv_sem):
@@ -591,9 +609,8 @@
         own = piece(design_b, z)
         chunks = [(to_third_b[i:j], to_even_b[i:j]) for i, j in zip(EDGES, EDGES[1:])]
         late_b = to_third_b[EDGES[1]:]
-        own_gram = dot(design_b, design_b, ((0,), (0,)))
-        moment = dot(target_blk[None, :], design_b)
-        part = pair_gram(True, (own,), (low_a,), (own_gram, moment))
+        part = own_gram(design_b, target_blk)
+        part = pair_gram(True, own, low_a, part)
         low_a, low_b, near_c, near_d, part, chunks = lax.optimization_barrier(
             (low_a, low_b, near_c, near_d, part, chunks))
         far_c, far_d = [], []
@@ -604,7 +621,7 @@
 
         send_late(chunks[0])
         high_b0 = swap(chunks[0][0], 2, 3)
-        part = pair_gram(True, (to_even,), (low_b,), (part,))
+        part = pair_gram(True, to_even, low_b, part)
         mine = stack_planes(part, 1)
         mine, late_b, chunks = lax.optimization_barrier((mine, late_b, chunks))
         send_late(chunks[1])
@@ -616,10 +633,10 @@
         own_b, near_c, up_low = lax.optimization_barrier((own, near_c, up_low))
         cross = cross_gram(True, 0, own_b, low_a, high_a, near_c, near_d)
         cross = cross_gram(False, EDGES[0], own_b, low_a, high_a, far_c[0], far_d[0], cross)
-        pair_high = pair_gram(False, (to_even,), (high_b0,), ())
+        pair_high = pair_gram(False, to_even, high_b0, jnp.zeros((8, BLOCK), F32))
         cross = cross_gram(False, EDGES[1], own_b, low_a, high_a, far_c[1], far_d[1], cross)
         high_b1, cross = lax.optimization_barrier((high_b1, cross))
-        pair_high = pair_gram(False, (to_even,), (high_b1,), (pair_high,), EDGES[1])
+        pair_high = pair_gram(False, to_even, high_b1, pair_high, EDGES[1])
         cross = cross_gram(False, EDGES[2], own_b, low_a, high_a, far_c[2], far_d[2], cross, pair_high)
         cross = sum_all(cross, 4)
         x_row, fits = factor_high(planes, ridge_cell, up_low, inv_low, cross, design_b)

time: 493 us -> 498 us (1.010)
  Pallas kernels: 243 us -> 279 us
  matrix products: 30.3 us -> 0 us
  starting transfers between devices: 61.3 us -> 52.5 us
    pallas_call x4 -> x5, Pallas kernels: 17.3 us -> 51.5 us  [the longest x1 32.7 us: own_gram(): pl.pallas_call(own_kernel, out_shape=jax.ShapeDtypeStruct((PAIR + EXTRA,...]
    dot_general x2 -> x0, matrix products: 30.3 us -> none  [dot(): lax.dot_general(a, b, (dims, ((), ())), precision=HIGHEST, preferred_elem...]
    ppermute x13, starting transfers between devices: 61.3 us -> 52.5 us  [swap(): return lax.ppermute(block, ('tp', 'dp'), pairs)]
  transfers between devices with their start and end apart: 13 -> 13, of which waited for: 5 -> 4; matrix products, arithmetic and copies ran while one was open for 10% -> 3% of each run, Pallas kernels for 28% -> 35%
where the time goes in v1:
time: 498 us; the launch traced here: 491 us
  Pallas kernels  279 us (56%)
  waiting for transfers between devices  127 us (26%)
  starting transfers between devices  52.5 us (11%)
  local copies, waits for them, and re-layouts  29.8 us (6%)
    ppermute x13, waiting for transfers between devices, swap(): return lax.ppermute(block, ('tp', 'dp'), pairs)  127 us
    pallas_call x3, Pallas kernels, comm_call(): pl.pallas_call(functools.partial(body, rows), out_shape=jax.ShapeDtypeStr...  115 us
    ppermute x13, starting transfers between devices, swap(): return lax.ppermute(block, ('tp', 'dp'), pairs)  52.5 us
    pallas_call x1, Pallas kernels, factor_high(): pl.pallas_call(high_kernel, out_shape=(jax.ShapeDtypeStruct((1, 2 * PAIR)...  41.8 us
    pallas_call x4, Pallas kernels, cross_gram(): pl.pallas_call(functools.partial(cross_kernel, early, pair is not None, p...  35.1 us
    pallas_call x1, Pallas kernels, own_gram(): pl.pallas_call(own_kernel, out_shape=jax.ShapeDtypeStruct((PAIR + EXTRA,...  32.7 us
    pallas_call x1, Pallas kernels, factor_low(): pl.pallas_call(low_kernel, out_shape=(jax.ShapeDtypeStruct((PAIR, PAIR +...  27.7 us
    pallas_call x4, Pallas kernels, pair_gram(): pl.pallas_call(functools.partial(pair_kernel, low), out_shape=jax.ShapeDt...  18.8 us
  transfers between devices with their start and end apart: 13, of which 4 were waited for; matrix products, arithmetic and copies ran while one was open for 3% of the time, Pallas kernels for 35%

profile of v1, /device:TPU:0, one launch (start us, length us, event | category | flops | bytes accessed | tf_op | source)
XLA Modules:
  0.0 491.3 jit_solution(2161906494997923982)
XLA Ops:
  0.6 3.8 constant_dynamic-slice_fusion.3
  4.5 3.8 constant_dynamic-slice_fusion.2
  8.2 4.9 %collective-permute-start.1 = (f32[2048,384]{1,0:T(8,128)}, f32[2048,384]{1,0:T(8,128)}, u32[]{:S(2)}, u32[]{:S(2)}) collective-permute-start(f32[2048,384]{1,0:T(8,128)} %constant_dynamic-slice_fusion.2), channel_id=1, source_target_pairs={{0,8},{1,9},{2,10},{3,11},{4,12},{5,13},{6,14},{7,15},{8,0},{9,1},... | collective-permute-start | bytes 9437192 | tf_op jit(solution)/shard_map/ppermute | solution.py:588
  15.5 3.5 collective-permute-start
  38.5 4.6 copy-done
  43.1 32.7 %own_gram.1.head = f32[896,384]{1,0:T(8,128)S(1)} custom-call(f32[8192,384]{1,0:T(8,128)S(1)} %copy-done, f32[32,1,256]{2,1,0:T(1,128)S(1)} %bitcast.7), custom_call_target="tpu_custom_call" | custom-call | flops 30000001024 | bytes 13000000 | tf_op jit(solution)/shard_map/own_gram/pallas_call | solution.py:508
  75.8 73.2 %collective-permute-done.mate.mate_lo = f32[2048,384]{1,0:T(8,128)} collective-permute-done((f32[2048,384]{1,0:T(8,128)}, f32[2048,384]{1,0:T(8,128)}, u32[]{:S(2)}, u32[]{:S(2)}) %collective-permute-start) | collective-permute-done | bytes 3145760 | tf_op jit(solution)/shard_map/ppermute | solution.py:588
  149.0 9.2 %pair_gram.4.head = f32[896,384]{1,0:T(8,128)S(1)} custom-call(f32[2048,384]{1,0:T(8,128)S(1)} %constant_dynamic-slice_fusion.near.own, f32[2048,384]{1,0:T(8,128)} %collective-permute-done.mate.mate_lo, f32[896,384]{1,0:T(8,128)S(1)} %own_gram.1.head), custom_call_target="tpu_custom_call" | custom-call | flops 6144000000 | bytes 12288000 | tf_op jit(solution)/shard_map/pair_gram/pallas_call | solution.py:541
  160.9 9.3 %pair_gram.5.part = f32[896,384]{1,0:T(8,128)S(1)} custom-call(f32[2048,384]{1,0:T(8,128)S(1)} %constant_dynamic-slice_fusion.1.near, f32[2048,384]{1,0:T(8,128)} %collective-permute-done.1.mate, f32[896,384]{1,0:T(8,128)S(1)} %pair_gram.4.head), custom_call_target="tpu_custom_call" | custom-call | flops 6144000000 | bytes 12288000 | tf_op jit(solution)/shard_map/pair_gram/pallas_call | solution.py:541
  170.2 38.8 %shard_map.50.mine = f32[4,112,384]{2,1,0:T(8,128)S(1)} custom-call(f32[896,384]{1,0:T(8,128)S(1)} %pair_gram.5.part), custom_call_target="tpu_custom_call" | custom-call | flops 1792000 | bytes 80000000 | tf_op jit(solution)/shard_map/pallas_call | solution.py:282
  211.0 27.5 %shard_map.51.planes = f32[4,896,384]{2,1,0:T(8,128)S(1)} custom-call(f32[4,112,384]{2,1,0:T(8,128)S(1)} %shard_map.50.mine), custom_call_target="tpu_custom_call" | custom-call | flops 1792000 | bytes 80000000 | tf_op jit(solution)/shard_map/pallas_call | solution.py:282
  239.5 27.7 %factor_low.1 = (f32[768,896]{1,0:T(8,128)S(1)}, f32[3,256,256]{2,1,0:T(8,128)S(1)}) custom-call(f32[4,896,384]{2,1,0:T(8,128)S(1)} %shard_map.51.planes, f32[1,1]{1,0:T(1,128)} %bitcast.4.ridge), custom_call_target="tpu_custom_call" | custom-call | flops 40000000000 | bytes 10000000 | tf_op jit(solution)/shard_map/factor_low/pallas_call | solution.py:390
  268.8 7.4 %collective-permute-start.8 = (f32[1024,384]{1,0:T(8,128)}, f32[1024,384]{1,0:T(8,128)S(1)}, u32[]{:S(2)}, u32[]{:S(2)}) collective-permute-start(f32[1024,384]{1,0:T(8,128)} %slice.23), channel_id=1, source_target_pairs={{0,24},{1,25},{2,26},{3,27},{4,28},{5,29},{6,30},{7,31},{24,0},{25... | collective-permute-start | bytes 4718600 | tf_op jit(solution)/shard_map/ppermute | solution.py:588
  278.1 6.9 %cross_gram.4.refs_0_ = f32[2048,384]{1,0:T(8,128)S(1)} custom-call(f32[2048,384]{1,0:T(8,128)S(1)} %constant_dynamic-slice_fusion.near.own, f32[2048,384]{1,0:T(8,128)} %collective-permute-done.mate.mate_lo, f32[2048,384]{1,0:T(8,128)} %collective-permute-done.4.mate_hi, f32[2048,384]{1,0:T(8,128)} %collective-permute-done.2.far_c, ...), custom_call_target="tpu_custom_call" | custom-call | flops 12288000000 | bytes 16384000 | tf_op jit(solution)/shard_map/cross_gram/pallas_call | solution.py:483
  285.1 16.8 %collective-permute-start.5 = (f32[512,384]{1,0:T(8,128)}, f32[512,384]{1,0:T(8,128)S(1)}, u32[]{:S(2)}, u32[]{:S(2)}) collective-permute-start(f32[512,384]{1,0:T(8,128)} %get-tuple-element.57), channel_id=1, source_target_pairs={{0,24},{1,25},{2,26},{3,27},{4,28},{5,29},{6,30},{7,31},{24,0},{25... | collective-permute-start | bytes 2359304 | tf_op jit(solution)/shard_map/ppermute | solution.py:588
  302.0 5.3 %collective-permute-start.6 = (f32[512,384]{1,0:T(8,128)S(1)}, f32[512,384]{1,0:T(8,128)S(1)}, u32[]{:S(2)}, u32[]{:S(2)}) collective-permute-start(f32[512,384]{1,0:T(8,128)S(1)} %copy-done.6), channel_id=1, source_target_pairs={{0,16},{1,17},{2,18},{3,19},{4,20},{5,21},{6,22},{7,23},{16,0},{17... | collective-permute-start | bytes 2359304 | tf_op jit(solution)/shard_map/ppermute | solution.py:588
  307.3 7.4 %cross_gram.5.refs_0_ = f32[2048,384]{1,0:T(8,128)S(1)} custom-call(f32[2048,384]{1,0:T(8,128)S(1)} %constant_dynamic-slice_fusion.near.own, f32[2048,384]{1,0:T(8,128)} %collective-permute-done.mate.mate_lo, f32[2048,384]{1,0:T(8,128)} %collective-permute-done.4.mate_hi, f32[512,384]{1,0:T(8,128)S(1)} %collective-permute-done.10.far_c, ...), custom_call_target="tpu_custom_call" | custom-call | flops 3072000000 | bytes 4096000 | tf_op jit(solution)/shard_map/cross_gram/pallas_call | solution.py:483
  314.7 16.1 %collective-permute-done.8.far_c = f32[1024,384]{1,0:T(8,128)S(1)} collective-permute-done((f32[1024,384]{1,0:T(8,128)}, f32[1024,384]{1,0:T(8,128)S(1)}, u32[]{:S(2)}, u32[]{:S(2)}) %collective-permute-start.8) | collective-permute-done | bytes 1572896 | tf_op jit(solution)/shard_map/ppermute | solution.py:588
  330.8 36.0 %collective-permute-done.9.far_d = f32[1024,384]{1,0:T(8,128)S(1)} collective-permute-done((f32[1024,384]{1,0:T(8,128)S(1)}, f32[1024,384]{1,0:T(8,128)S(1)}, u32[]{:S(2)}, u32[]{:S(2)}) %collective-permute-start.9) | collective-permute-done | bytes 1572896 | tf_op jit(solution)/shard_map/ppermute | solution.py:588
  366.8 13.4 %cross_gram.6.refs_1_ = f32[2048,384]{1,0:T(8,128)S(1)} custom-call(f32[2048,384]{1,0:T(8,128)S(1)} %constant_dynamic-slice_fusion.near.own, f32[2048,384]{1,0:T(8,128)} %collective-permute-done.mate.mate_lo, f32[2048,384]{1,0:T(8,128)} %collective-permute-done.4.mate_hi, f32[1024,384]{1,0:T(8,128)S(1)} %collective-permute-done.8.far_c, ...), custom_call_target="tpu_custom_call" | custom-call | flops 6144000000 | bytes 8192000 | tf_op jit(solution)/shard_map/cross_gram/pallas_call | solution.py:483
  382.5 7.4 %cross_gram.7.part = f32[2048,384]{1,0:T(8,128)S(1)} custom-call(f32[2048,384]{1,0:T(8,128)S(1)} %constant_dynamic-slice_fusion.near.own, f32[2048,384]{1,0:T(8,128)} %collective-permute-done.mate.mate_lo, f32[2048,384]{1,0:T(8,128)} %collective-permute-done.4.mate_hi, f32[512,384]{1,0:T(8,128)S(1)} %collective-permute-done.5.far_c, ...), custom_call_target="tpu_custom_call" | custom-call | flops 3072000000 | bytes 4096000 | tf_op jit(solution)/shard_map/cross_gram/pallas_call | solution.py:483
  389.9 48.4 %shard_map.52.cross = f32[1,2048,384]{2,1,0:T(8,128)S(1)} custom-call(f32[2048,384]{1,0:T(8,128)S(1)} %cross_gram.7.part), custom_call_target="tpu_custom_call" | custom-call | flops 4096000 | bytes 80000000 | tf_op jit(solution)/shard_map/pallas_call | solution.py:282
  438.4 41.8 %factor_high.1 = (f32[1,1536]{1,0:T(1,128)S(1)}, f32[64,128]{1,0:T(8,128)S(1)}) custom-call(f32[4,896,384]{2,1,0:T(8,128)S(1)} %shard_map.51.planes, f32[1,1]{1,0:T(1,128)} %bitcast.5.ridge, f32[768,896]{1,0:T(8,128)S(1)} %copy-done.4, f32[3,256,256]{2,1,0:T(8,128)S(1)} %get-tuple-element.54.inv_low, f32[1,2048,384]{2,1,0:T(8,128)S(1)} %shard_map.52.cross, ...), custom_call_target="tpu_custom_call" | custom-call | flops 49999998976 | bytes 10000000 | tf_op jit(solution)/shard_map/factor_high/pallas_call | solution.py:405
  480.8 8.3 %residual.1 = f32[64,128]{1,0:T(8,128)} custom-call(f32[64,128]{1,0:T(8,128)} %copy-done.2, f32[64,128]{1,0:T(8,128)} %bitcast.6), custom_call_target="tpu_custom_call" | custom-call | flops 3000000000 | bytes 1000000 | tf_op jit(solution)/shard_map/residual/pallas_call | solution.py:568
  (42 shorter events, 35.2 us)
Async XLA Ops:
  8.2 150.0 %collective-permute-start.1 = (f32[2048,384]{1,0:T(8,128)}, f32[2048,384]{1,0:T(8,128)}, u32[]{:S(2)}, u32[]{:S(2)}) collective-permute-start(f32[2048,384]{1,0:T(8,128)} %constant_dynamic-slice_fusion.2), channel_id=1, source_target_pairs={{0,8},{1,9},{2,10},{3,11},{4,12},{5,13},{6,14},{7,15},{8,0},{9,1},... | collective-permute-start | bytes 9437192 | tf_op jit(solution)/shard_map/ppermute | solution.py:588
  13.2 145.1 %collective-permute-start.2 = (f32[2048,384]{1,0:T(8,128)}, f32[2048,384]{1,0:T(8,128)}, u32[]{:S(2)}, u32[]{:S(2)}) collective-permute-start(f32[2048,384]{1,0:T(8,128)} %constant_dynamic-slice_fusion.2), channel_id=1, source_target_pairs={{8,16},{9,17},{10,18},{11,19},{12,20},{13,21},{14,22},{15,23},{16,... | collective-permute-start | bytes 9437192 | tf_op jit(solution)/shard_map/ppermute | solution.py:588
  15.5 133.5 %collective-permute-start = (f32[2048,384]{1,0:T(8,128)}, f32[2048,384]{1,0:T(8,128)}, u32[]{:S(2)}, u32[]{:S(2)}) collective-permute-start(f32[2048,384]{1,0:T(8,128)} %constant_dynamic-slice_fusion.3), channel_id=1, source_target_pairs={{0,8},{1,9},{2,10},{3,11},{4,12},{5,13},{6,14},{7,15},{8,0},{9,1},... | collective-permute-start | bytes 9437192 | tf_op jit(solution)/shard_map/ppermute | solution.py:588
  19.0 249.7 %collective-permute-start.4 = (f32[2048,384]{1,0:T(8,128)}, f32[2048,384]{1,0:T(8,128)}, u32[]{:S(2)}, u32[]{:S(2)}) collective-permute-start(f32[2048,384]{1,0:T(8,128)} %constant_dynamic-slice_fusion.3), channel_id=1, source_target_pairs={{16,24},{17,25},{18,26},{19,27},{20,28},{21,29},{22,30},{23,31},{2... | collective-permute-start | bytes 9437192 | tf_op jit(solution)/shard_map/ppermute | solution.py:588
  23.5 134.8 %collective-permute-start.3 = (f32[2048,384]{1,0:T(8,128)S(1)}, f32[2048,384]{1,0:T(8,128)}, u32[]{:S(2)}, u32[]{:S(2)}) collective-permute-start(f32[2048,384]{1,0:T(8,128)S(1)} %constant_dynamic-slice_fusion.1.near), channel_id=1, source_target_pairs={{8,24},{9,25},{10,26},{11,27},{12,28},{13,29},{14,30},{15,31},{24,... | collective-permute-start | bytes 9437192 | tf_op jit(solution)/shard_map/ppermute | solution.py:588
  35.7 2.7 copy-start.1
  38.5 4.6 copy-start
  158.3 126.9 %collective-permute-start.10 = (f32[512,384]{1,0:T(8,128)S(1)}, f32[512,384]{1,0:T(8,128)S(1)}, u32[]{:S(2)}, u32[]{:S(2)}) collective-permute-start(f32[512,384]{1,0:T(8,128)S(1)} %get-tuple-element.44), channel_id=1, source_target_pairs={{0,24},{1,25},{2,26},{3,27},{4,28},{5,29},{6,30},{7,31},{24,0},{25... | collective-permute-start | bytes 2359304 | tf_op jit(solution)/shard_map/ppermute | solution.py:588
  160.2 115.9 %collective-permute-start.12 = (f32[512,384]{1,0:T(8,128)S(1)}, f32[512,384]{1,0:T(8,128)S(1)}, u32[]{:S(2)}, u32[]{:S(2)}) collective-permute-start(f32[512,384]{1,0:T(8,128)S(1)} %get-tuple-element.44), channel_id=1, source_target_pairs={{16,24},{17,25},{18,26},{19,27},{20,28},{21,29},{22,30},{23,31},{2... | collective-permute-start | bytes 2359304 | tf_op jit(solution)/shard_map/ppermute | solution.py:588
  209.0 92.9 %collective-permute-start.11 = (f32[512,384]{1,0:T(8,128)S(1)}, f32[512,384]{1,0:T(8,128)S(1)}, u32[]{:S(2)}, u32[]{:S(2)}) collective-permute-start(f32[512,384]{1,0:T(8,128)S(1)} %get-tuple-element.45), channel_id=1, source_target_pairs={{0,16},{1,17},{2,18},{3,19},{4,20},{5,21},{6,22},{7,23},{16,0},{17... | collective-permute-start | bytes 2359304 | tf_op jit(solution)/shard_map/ppermute | solution.py:588
  238.4 141.8 %collective-permute-start.7 = (f32[1536,384]{1,0:T(8,128)}, f32[1536,384]{1,0:T(8,128)S(1)}, u32[]{:S(2)}, u32[]{:S(2)}) collective-permute-start(f32[1536,384]{1,0:T(8,128)} %slice.27), channel_id=1, source_target_pairs={{16,24},{17,25},{18,26},{19,27},{20,28},{21,29},{22,30},{23,31},{2... | collective-permute-start | bytes 7077896 | tf_op jit(solution)/shard_map/ppermute | solution.py:588
  239.5 36.6 %copy-start.5 = (f32[1024,384]{1,0:T(8,128)S(1)}, f32[1024,384]{1,0:T(8,128)}, u32[]{:S(2)}) copy-start(f32[1024,384]{1,0:T(8,128)} %slice.24) | copy-start | bytes 4718596
  267.2 1.5 copy-start.3
  268.8 62.0 %collective-permute-start.8 = (f32[1024,384]{1,0:T(8,128)}, f32[1024,384]{1,0:T(8,128)S(1)}, u32[]{:S(2)}, u32[]{:S(2)}) collective-permute-start(f32[1024,384]{1,0:T(8,128)} %slice.23), channel_id=1, source_target_pairs={{0,24},{1,25},{2,26},{3,27},{4,28},{5,29},{6,30},{7,31},{24,0},{25... | collective-permute-start | bytes 4718600 | tf_op jit(solution)/shard_map/ppermute | solution.py:588
  276.2 90.6 %collective-permute-start.9 = (f32[1024,384]{1,0:T(8,128)S(1)}, f32[1024,384]{1,0:T(8,128)S(1)}, u32[]{:S(2)}, u32[]{:S(2)}) collective-permute-start(f32[1024,384]{1,0:T(8,128)S(1)} %copy-done.5), channel_id=1, source_target_pairs={{0,16},{1,17},{2,18},{3,19},{4,20},{5,21},{6,22},{7,23},{16,0},{17... | collective-permute-start | bytes 4718600 | tf_op jit(solution)/shard_map/ppermute | solution.py:588
  285.0 17.0 %copy-start.6 = (f32[512,384]{1,0:T(8,128)S(1)}, f32[512,384]{1,0:T(8,128)}, u32[]{:S(2)}) copy-start(f32[512,384]{1,0:T(8,128)} %get-tuple-element.58) | copy-start | bytes 2359300
  285.1 95.3 %collective-permute-start.5 = (f32[512,384]{1,0:T(8,128)}, f32[512,384]{1,0:T(8,128)S(1)}, u32[]{:S(2)}, u32[]{:S(2)}) collective-permute-start(f32[512,384]{1,0:T(8,128)} %get-tuple-element.57), channel_id=1, source_target_pairs={{0,24},{1,25},{2,26},{3,27},{4,28},{5,29},{6,30},{7,31},{24,0},{25... | collective-permute-start | bytes 2359304 | tf_op jit(solution)/shard_map/ppermute | solution.py:588
  302.0 80.5 %collective-permute-start.6 = (f32[512,384]{1,0:T(8,128)S(1)}, f32[512,384]{1,0:T(8,128)S(1)}, u32[]{:S(2)}, u32[]{:S(2)}) collective-permute-start(f32[512,384]{1,0:T(8,128)S(1)} %copy-done.6), channel_id=1, source_target_pairs={{0,16},{1,17},{2,18},{3,19},{4,20},{5,21},{6,22},{7,23},{16,0},{17... | collective-permute-start | bytes 2359304 | tf_op jit(solution)/shard_map/ppermute | solution.py:588
  389.9 48.4 %copy-start.4 = (f32[768,896]{1,0:T(8,128)S(1)}, f32[768,896]{1,0:T(8,128)}, u32[]{:S(2)}) copy-start(f32[768,896]{1,0:T(8,128)} %copy-done.3) | copy-start | bytes 8257540
  480.1 0.6 copy-start.2
